TPU v7x, 32 devices: a whole 2x2x4 slice. The times are simulated.
32 devices in a mesh: grp: 2 (over y), row: 16 (over z, x, core).
Axes of the slice: x: 2, y: 2, z: 4, core: 2. Of those that a mesh axis runs over, the one named last changes fastest.
Arguments:
- item_ids: int32 [128, 512], P(('grp', 'row')), may hold values from 0 to 49999, as said below
- lengths: int32 [128], P(('grp', 'row')), may hold values from 358 to 512
- target_ids: int32 [128, 512], P(('grp', 'row')), may hold values from 0 to 49999
- target_logq: bfloat16 [128, 512], P(('grp', 'row')), may hold values from -4 to 0
- negative_ids: int32 [2048], P(('grp', 'row')), may hold values from 0 to 49999
- negative_logq: bfloat16 [2048], P(('grp', 'row')), may hold values from -4 to 0
- table_weight: float32 [50000, 256], P('row'), may hold values from -0.6 to 0.6
- table_accum: float32 [50000], P('row'), may hold values from 1.1737531e-13 to 4.6950123e-13
- dense_weight: float32 [256, 4608], P(None, ('grp', 'row')), may hold values from -0.375 to 0.375
- dense_first: float32 [256, 4608], P(None, ('grp', 'row')), may hold values from -2.861023e-06 to 2.861023e-06
- dense_second: float32 [256, 4608], P(None, ('grp', 'row')), may hold values from 3.390842e-15 to 1.3563368e-14
- gain_weight: float32 [3, 256], replicated, may hold values from 0.5 to 1.5
- gain_first: float32 [3, 256], replicated, may hold values from -3.0517578e-05 to 3.0517578e-05
- gain_second: float32 [3, 256], replicated, may hold values from 3.390842e-13 to 1.3563368e-12
Outputs:
- mean_loss: float32 [], replicated
- grad_norm: float32 [], replicated
- new_table: float32 [50000, 256], P('row')
- table_grad: float32 [50000, 256], P('row')
- new_accum: float32 [50000], P('row')
- table_copy: bfloat16 [50000, 256], P('row')
- new_dense: float32 [256, 4608], P(None, ('grp', 'row'))
- new_first: float32 [256, 4608], P(None, ('grp', 'row'))
- new_second: float32 [256, 4608], P(None, ('grp', 'row'))
- dense_copy: bfloat16 [256, 4608], P(None, ('grp', 'row'))
- new_gains: float32 [3, 256], replicated
- new_gain_first: float32 [3, 256], replicated
- new_gain_second: float32 [3, 256], replicated
Inputs may be any that keep to these rules, and one draw needn't show every extreme that they name: `item_ids`: taking one device's item ids, target ids and negative ids together, at most 520 of them name rows with the same id // 3125; in each group some value of id // 3125 is named exactly 520 times by every device of the group.
All inputs are finite; a program needn't handle non-finite values.
Results may differ from a plain program's by a relative error of at most 0.0093.
The roundings to bfloat16 on the way count: a program that leaves them out, or rounds other values in their place, can miss the bound.
Values may be sent and summed in bfloat16 or wider, within the bound.
A program may use at most 256 MiB of HBM per device.

v0:
```python
import jax
import jax.numpy as jnp
from jax import lax
from jax.sharding import PartitionSpec as P

HEADS = 8
HDIM = 64
FF = 1024
STEP = 10
clip_level = 0.002
adam_rate = 0.05
gains_rate = 0.6
rows_rate = 0.05
beta_one = 0.9
beta_two = 0.999
adam_eps = 1e-08
decay_rate = 0.01


def in_blocks(array, dim, devices):
    shape = array.shape
    pieces = array.reshape(*shape[:dim], devices, shape[dim] // devices, *shape[dim + 1 :])
    return jnp.moveaxis(pieces, dim, 0)


def sum_at_owner(array, axis, dim):
    devices = lax.axis_size(axis)
    pieces = lax.all_to_all(in_blocks(array, dim, devices), axis, 0, 0, tiled=True)
    return jnp.sum(pieces.astype(jnp.float32), axis=0)


def norm_apply(values, gain):
    return values * lax.rsqrt(jnp.mean(values * values, -1, keepdims=True) + 1e-06) * gain


def gelu_apply(values):
    return jax.nn.gelu(values, approximate=True)


def adam_update(weight, first, second, grad, decay, rate):
    first_new = beta_one * first + (1.0 - beta_one) * grad
    second_new = beta_two * second + (1.0 - beta_two) * grad * grad
    fix_one = 1.0 - beta_one**STEP
    fix_two = 1.0 - beta_two**STEP
    weight_new = weight - rate * (
        first_new / fix_one / (jnp.sqrt(second_new / fix_two) + adam_eps) + decay * weight
    )
    return (weight_new, first_new, second_new)


def attention_probs(queries, keys_all):
    scores = (
        jnp.einsum("sqhd,skhd->shqk", queries, keys_all, preferred_element_type=jnp.float32) * 0.125
    )
    length = queries.shape[1]
    causal = lax.broadcasted_iota(jnp.int32, (length, length), 0) >= lax.broadcasted_iota(
        jnp.int32, (length, length), 1
    )
    scores = jnp.where(causal[None, None], scores, -1e30)
    exponent = jnp.exp(scores - jnp.max(scores, -1, keepdims=True))
    return exponent / jnp.sum(exponent, -1, keepdims=True)


def shards(
    item_ids,
    lengths,
    target_ids,
    target_logq,
    negative_ids,
    negative_logq,
    table_weight,
    table_accum,
    dense_weight,
    dense_first,
    dense_second,
    gain_weight,
    gain_first,
    gain_second,
):
    seq_dev, length = item_ids.shape
    rows_dev, model_width = table_weight.shape
    peer_count = lax.axis_size("row")
    inner = HEADS * HDIM
    tokens = seq_dev * length
    single_float = jnp.float32
    brain_float_half = jnp.bfloat16
    local_dense = dense_weight.astype(brain_float_half)
    full_dense = lax.all_gather(local_dense, ("grp", "row"), axis=1, tiled=True)
    query_key_value_weight = full_dense[:, : 3 * inner]
    output_weight = full_dense[:, 3 * inner : 4 * inner]
    up_weight = full_dense[:, 4 * inner : 4 * inner + FF]
    down_weight = full_dense[:, 4 * inner + FF : 4 * inner + 2 * FF]
    pos_rows = full_dense[:, 4 * inner + 2 * FF :].T.astype(single_float)
    requests = jnp.concatenate([item_ids.reshape(-1), target_ids.reshape(-1), negative_ids])
    capacity = 2 * requests.shape[0] // peer_count
    owners = requests // rows_dev
    one_hot = (owners[:, None] == jnp.arange(peer_count, dtype=jnp.int32)[None, :]).astype(
        jnp.int32
    )
    rank_in = jnp.sum((jnp.cumsum(one_hot, 0) - one_hot) * one_hot, 1)
    slot_at = owners * capacity + rank_in
    send_ids = jnp.full((peer_count * capacity,), -1, jnp.int32).at[slot_at].set(requests)
    send_ids = send_ids.reshape(peer_count, capacity)
    table_low = table_weight.astype(brain_float_half)
    row_base = lax.axis_index("row") * rows_dev
    asked_ids = lax.all_to_all(send_ids, "row", split_axis=0, concat_axis=0, tiled=True)
    present = asked_ids >= 0
    found_rows = table_low[jnp.where(present, asked_ids - row_base, 0)]
    found_rows = jnp.where(present[..., None], found_rows, jnp.zeros_like(found_rows))
    returned = lax.all_to_all(found_rows, "row", split_axis=0, concat_axis=0, tiled=True)
    fetched, asked_ids = (returned, asked_ids)
    picked = fetched.reshape(peer_count * capacity, model_width)[slot_at]
    hist_rows = picked[:tokens].reshape(seq_dev, length, model_width)
    target_rows = picked[tokens : 2 * tokens]
    own_negatives = picked[2 * tokens :]
    neg_rows, neg_bias = (
        lax.all_gather(own_negatives, "row", axis=0, tiled=True),
        lax.all_gather(negative_logq, "row", axis=0, tiled=True),
    )
    embedded_tokens = hist_rows.astype(single_float) + pos_rows[None]
    normed, norm_back_one = jax.vjp(norm_apply, embedded_tokens, gain_weight[0])
    normalized_narrow = normed.astype(brain_float_half)
    mixed_state = jnp.einsum(
        "rnq,qm->rnm",
        normalized_narrow,
        query_key_value_weight,
        preferred_element_type=single_float,
    ).astype(brain_float_half)
    queries = mixed_state[..., :inner].reshape(seq_dev, length, HEADS, HDIM)
    keys_all = mixed_state[..., inner : 2 * inner].reshape(seq_dev, length, HEADS, HDIM)
    values_all = mixed_state[..., 2 * inner :].reshape(seq_dev, length, HEADS, HDIM)
    attn_probs = attention_probs(queries, keys_all)
    probs_low = attn_probs.astype(brain_float_half)
    attention_context = jnp.einsum(
        "shqk,skhd->sqhd", probs_low, values_all, preferred_element_type=single_float
    )
    attention_context = attention_context.reshape(seq_dev, length, inner).astype(brain_float_half)
    after_attention_state = embedded_tokens + jnp.einsum(
        "xaj,oj->xao", attention_context, output_weight, preferred_element_type=single_float
    )
    normed_two, norm_back_two = jax.vjp(norm_apply, after_attention_state, gain_weight[1])
    second_normalized_narrow = normed_two.astype(brain_float_half)
    hidden_preactivation = jnp.einsum(
        "bvi,iq->bvq", second_normalized_narrow, up_weight, preferred_element_type=single_float
    )
    hidden, gaussian_unit_backward = jax.vjp(gelu_apply, hidden_preactivation)
    hidden_narrow = hidden.astype(brain_float_half)
    after_ffn = after_attention_state + jnp.einsum(
        "ixn,on->ixo", hidden_narrow, down_weight, preferred_element_type=single_float
    )
    states, norm_back_three = jax.vjp(norm_apply, after_ffn, gain_weight[2])
    states_low = states.astype(brain_float_half).reshape(tokens, model_width)
    states_full = states_low.astype(single_float)
    target_full = target_rows.astype(single_float)
    pos_logit = jnp.sum(states_full * target_full, -1) - target_logq.reshape(tokens).astype(
        single_float
    )
    neg_logit = (
        jnp.einsum("td,nd->tn", states_low, neg_rows, preferred_element_type=single_float)
        - neg_bias.astype(single_float)[None, :]
    )
    highest_logit = jnp.maximum(jnp.max(neg_logit, 1), pos_logit)
    log_total = highest_logit + jnp.log(
        jnp.exp(pos_logit - highest_logit) + jnp.sum(jnp.exp(neg_logit - highest_logit[:, None]), 1)
    )
    is_valid = lax.broadcasted_iota(jnp.int32, (seq_dev, length), 1) < lengths[:, None]
    valid_full = is_valid.reshape(tokens).astype(single_float)
    loss_local = jnp.sum(valid_full * (log_total - pos_logit))
    event_local = jnp.sum(valid_full)
    loss_total, event_total = lax.psum((loss_local, event_local), ("grp", "row"))
    inverse = 1.0 / event_total
    d_pos = valid_full * inverse * (jnp.exp(pos_logit - log_total) - 1.0)
    d_neg = (valid_full[:, None] * inverse * jnp.exp(neg_logit - log_total[:, None])).astype(
        brain_float_half
    )
    d_states = d_pos[:, None] * target_full + jnp.einsum(
        "tn,nd->td", d_neg, neg_rows, preferred_element_type=single_float
    )
    d_target = d_pos[:, None] * states_full
    neg_grad = sum_at_owner(
        jnp.einsum("tn,td->nd", d_neg, states_low, preferred_element_type=single_float).astype(
            jnp.bfloat16
        ),
        "row",
        0,
    )
    d_ffn, d_gain_three = norm_back_three(d_states.reshape(seq_dev, length, model_width))
    branch_gradient = d_ffn.astype(brain_float_half)
    down_weight_gradient = jnp.einsum(
        "qgp,qgv->pv", branch_gradient, hidden_narrow, preferred_element_type=single_float
    )
    (hidden_gradient,) = gaussian_unit_backward(
        jnp.einsum("bvi,iq->bvq", branch_gradient, down_weight, preferred_element_type=single_float)
    )
    hidden_gradient_narrow = hidden_gradient.astype(brain_float_half)
    up_weight_gradient = jnp.einsum(
        "qgp,qgv->pv",
        second_normalized_narrow,
        hidden_gradient_narrow,
        preferred_element_type=single_float,
    )
    d_attn_part, d_gain_two = norm_back_two(
        jnp.einsum(
            "ixn,on->ixo", hidden_gradient_narrow, up_weight, preferred_element_type=single_float
        )
    )
    d_attn = d_ffn + d_attn_part
    output_gradient_narrow = d_attn.astype(brain_float_half)
    output_weight_gradient = jnp.einsum(
        "nkg,nka->ga",
        output_gradient_narrow,
        attention_context,
        preferred_element_type=single_float,
    )
    context_gradient = jnp.einsum(
        "mbg,gr->mbr", output_gradient_narrow, output_weight, preferred_element_type=single_float
    ).astype(brain_float_half)
    context_gradient = context_gradient.reshape(seq_dev, length, HEADS, HDIM)
    d_values = jnp.einsum(
        "shqk,sqhd->skhd", probs_low, context_gradient, preferred_element_type=single_float
    )
    d_probs = jnp.einsum(
        "sqhd,skhd->shqk", context_gradient, values_all, preferred_element_type=single_float
    )
    d_scores = (attn_probs * (d_probs - jnp.sum(attn_probs * d_probs, -1, keepdims=True))).astype(
        brain_float_half
    )
    d_queries = (
        jnp.einsum("shqk,skhd->sqhd", d_scores, keys_all, preferred_element_type=single_float)
        * 0.125
    )
    d_keys = (
        jnp.einsum("shqk,sqhd->skhd", d_scores, queries, preferred_element_type=single_float)
        * 0.125
    )
    mixed_gradient = jnp.concatenate(
        [
            d_queries.reshape(seq_dev, length, inner),
            d_keys.reshape(seq_dev, length, inner),
            d_values.reshape(seq_dev, length, inner),
        ],
        -1,
    ).astype(brain_float_half)
    query_key_value_gradient = jnp.einsum(
        "rbp,rbg->pg", normalized_narrow, mixed_gradient, preferred_element_type=single_float
    )
    d_embed_part, d_gain_one = norm_back_one(
        jnp.einsum(
            "igp,zp->igz",
            mixed_gradient,
            query_key_value_weight,
            preferred_element_type=single_float,
        )
    )
    d_embedded = d_attn + d_embed_part
    grad_pos = jnp.sum(d_embedded, 0).T
    grad_local = jnp.concatenate(
        [
            query_key_value_gradient,
            output_weight_gradient,
            up_weight_gradient,
            down_weight_gradient,
            grad_pos,
        ],
        1,
    )
    gain_local = jnp.stack([d_gain_one, d_gain_two, d_gain_three])
    dense_grad = lax.psum_scatter(grad_local, ("grp", "row"), scatter_dimension=1, tiled=True)
    row_grads = jnp.concatenate([d_embedded.reshape(tokens, model_width), d_target, neg_grad], 0)
    sent_grads = (
        jnp.zeros((peer_count * capacity, model_width), single_float).at[slot_at].set(row_grads)
    )
    arrived = lax.all_to_all(
        sent_grads.reshape(peer_count, capacity, model_width).astype(jnp.bfloat16),
        "row",
        split_axis=0,
        concat_axis=0,
        tiled=True,
    ).astype(jnp.float32)
    present = asked_ids >= 0
    local_rows = jnp.where(present, asked_ids - row_base, 0).reshape(-1)
    arrived = jnp.where(present[..., None], arrived, 0.0).reshape(-1, model_width)
    owner_grad = jax.ops.segment_sum(arrived, local_rows, num_segments=rows_dev)
    table_full = lax.psum(owner_grad.astype(jnp.bfloat16), "grp").astype(jnp.float32)
    dense_sq = jnp.sum(dense_grad * dense_grad)
    table_sq = jnp.sum(table_full * table_full) / lax.axis_size("grp")
    gain_grad, dense_total, table_total = lax.psum((gain_local, dense_sq, table_sq), ("grp", "row"))
    raw_norm = jnp.sqrt(dense_total + table_total + jnp.sum(gain_grad * gain_grad))
    factor = jnp.minimum(1.0, clip_level / raw_norm)
    table_grad = table_full * factor
    new_accum = table_accum + jnp.mean(table_grad * table_grad, -1)
    new_table = table_weight - rows_rate * table_grad / (jnp.sqrt(new_accum)[:, None] + adam_eps)
    new_dense, new_first, new_second = adam_update(
        dense_weight, dense_first, dense_second, dense_grad * factor, decay_rate, adam_rate
    )
    new_gains, new_gain_first, new_gain_second = adam_update(
        gain_weight, gain_first, gain_second, gain_grad * factor, 0.0, gains_rate
    )
    mean_loss = loss_total / event_total
    return (
        mean_loss,
        raw_norm,
        new_table,
        table_grad,
        new_accum,
        new_table.astype(brain_float_half),
        new_dense,
        new_first,
        new_second,
        new_dense.astype(brain_float_half),
        new_gains,
        new_gain_first,
        new_gain_second,
    )


def solution(mesh):
    return jax.shard_map(
        shards,
        mesh=mesh,
        in_specs=(
            P(("grp", "row"), None),
            P(("grp", "row")),
            P(("grp", "row"), None),
            P(("grp", "row"), None),
            P(("grp", "row")),
            P(("grp", "row")),
            P("row", None),
            P("row"),
            P(None, ("grp", "row")),
            P(None, ("grp", "row")),
            P(None, ("grp", "row")),
            P(),
            P(),
            P(),
        ),
        out_specs=(
            P(),
            P(),
            P("row", None),
            P("row", None),
            P("row"),
            P("row", None),
            P(None, ("grp", "row")),
            P(None, ("grp", "row")),
            P(None, ("grp", "row")),
            P(None, ("grp", "row")),
            P(),
            P(),
            P(),
        ),
        check_vma=False,
    )
```

profile of v0, /device:TPU:0, one launch (start us, length us, event | category | flops | bytes accessed | tf_op | source)
XLA Modules:
  0.0 841.4 jit_solution(8096171434932233010)
XLA Ops:
  16.7 20.6 %scatter_custom_fusion = s32[8320]{0:T(1024)S(1)} fusion(s32[4160]{0:T(1024)S(1)} %fusion.57, s32[4160]{0:T(1024)S(1)} %constant_dynamic-update-slice_fusion.1, s32[]{:T(128)} %constant.34.clone.1), kind=kCustom, calls=%fused_computation.133 | custom fusion | bytes 33284 | tf_op jit(solution)/shard_map/scatter | solution.py:102
  38.0 7.4 all-to-all-start
  52.8 24.2 %gather_fusion = bf16[8320,256]{1,0:T(8,128)(2,1)} fusion(bf16[3125,256]{1,0:T(8,128)(2,1)S(1)} %convert_element_type.132, s32[9216]{0:T(1024)S(1)} %pad_clamp_fusion), kind=kCustom, calls=%fused_computation | custom fusion | bytes 8552960 | tf_op jit(solution)/shard_map/gather | solution.py:108
  89.9 99.9 %all-reduce.1 = bf16[1024]{0:T(1024)(128)(2,1)S(1)} all-reduce(bf16[1024]{0:T(1024)(128)(2,1)S(1)} %dynamic-update-slice), channel_id=1, replica_groups=mesh['grp'=2,'row'=16] {'row'}, use_global_device_ids=true, to_apply=%add.1 | all-reduce | flops 1024 | bytes 4096
  191.0 12.5 %gather_fusion.1 = bf16[4160,256]{1,0:T(8,128)(2,1)S(1)} fusion(bf16[8320,256]{1,0:T(8,128)(2,1)} %bitcast.5, s32[5120]{0:T(1024)S(1)} %pad_clamp_fusion.1), kind=kCustom, calls=%fused_computation.1 | custom fusion | bytes 4276480 | tf_op jit(solution)/shard_map/gather | solution.py:112
  205.6 40.4 %all_gather.10 = bf16[1024,256]{1,0:T(8,128)(2,1)} all-gather(bf16[64,256]{1,0:T(8,128)(2,1)S(1)} %slice.84), channel_id=1, replica_groups=mesh['grp'=2,'row'=16] {'row'}, dimensions={0}, use_global_device_ids=true | all-gather | bytes 557056 | tf_op jit(solution)/shard_map/all_gather | solution.py:117
  263.7 19.1 %fusion.72 = (f32[4,8,512]{2,1,0:T(8,128)S(1)}, f32[4,8,512,512]{2,3,1,0:T(8,128)}) fusion(pred[512,512]{0,1:T(8,128)(4,1)S(1)} %iota_compare_fusion, bf16[4,512,8,64]{1,3,2,0:T(8,128)(2,1)} %bitcast.183, bf16[4,512,8,64]{1,3,2,0:T(8,128)(2,1)S(1)} %bitcast.181), kind=kOutput, calls=%fused_computation.173 | convolution fusion | flops 1107296768 | bytes 38076416 | tf_op jit(solution)/shard_map/sub | solution.py:60
  282.8 14.4 %fusion.33 = bf16[4,8,64,512]{3,2,1,0:T(8,128)(2,1)} fusion(bf16[4,512,8,64]{1,3,2,0:T(8,128)(2,1)} %bitcast.193, f32[4,8,512,512]{2,3,1,0:T(8,128)} %get-tuple-element.102, f32[4,8,512]{2,1,0:T(8,128)S(1)} %get-tuple-element.101), kind=kOutput, calls=%fused_computation.78 | convolution fusion | flops 1091567616 | bytes 37814272 | tf_op jit(solution)/shard_map/shqk,skhd->sqhd/dot_general | solution.py:134
  321.2 38.9 %psum.43 = f32[]{:T(128)} all-reduce(f32[]{:T(128)} %get-tuple-element.71), channel_id=1, replica_groups=mesh['grp'=2,'row'=16] {'grp','row'}, use_global_device_ids=true, to_apply=%region_15.16 | all-reduce | flops 1 | bytes 8 | tf_op jit(solution)/shard_map/psum | solution.py:170
  373.8 6.7 fusion.11
  387.8 15.3 %fusion.36 = bf16[4,8,64,512]{3,2,1,0:T(8,128)(2,1)} fusion(bf16[4,512,8,64]{1,3,2,0:T(8,128)(2,1)} %bitcast.196, f32[4,8,512,512]{2,3,1,0:T(8,128)} %get-tuple-element.102, f32[4,8,512]{2,1,0:T(8,128)S(1)} %get-tuple-element.101), kind=kOutput, calls=%fused_computation.79 | convolution fusion | flops 1091567616 | bytes 37814272 | tf_op jit(solution)/shard_map/shqk,sqhd->skhd/dot_general | solution.py:219
  403.1 22.9 %multiply_reduce_fusion = (f32[4,8,512]{2,1,0:T(8,128)S(1)}, f32[4,8,512,512]{2,3,1,0:T(8,128)}) fusion(f32[4,8,512,512]{2,3,1,0:T(8,128)} %get-tuple-element.102, f32[4,8,512]{2,1,0:T(8,128)S(1)} %get-tuple-element.101, bf16[4,512,8,64]{1,3,2,0:T(8,128)(2,1)} %bitcast.197, bf16[4,512,8,64]{1,3,2,0:T(8,128)(2,1)} %bitcast.194), kind=kOutput, calls=%fused_computation.7 | convolution fusion | flops 1098891264 | bytes 71434240 | tf_op jit(solution)/shard_map/sqhd,skhd->shqk/dot_general | solution.py:222
  426.0 27.6 %multiply_convert_fusion = bf16[4,8,512,512]{2,3,1,0:T(8,128)(2,1)} fusion(f32[4,8,512,512]{2,3,1,0:T(8,128)} %get-tuple-element.111, f32[4,8,512]{2,1,0:T(8,128)S(1)} %get-tuple-element.110, f32[4,8,512,512]{2,3,1,0:T(8,128)} %get-tuple-element.102, f32[4,8,512]{2,1,0:T(8,128)S(1)} %get-tuple-element.101), kind=kLoop, calls=%fused_computation.6 | loop fusion | flops 33554432 | bytes 84017152 | tf_op jit(solution)/shard_map/convert_element_type | solution.py:225
  453.6 12.9 %multiply_convert_fusion.3 = bf16[4,8,64,512]{3,2,1,0:T(8,128)(2,1)} fusion(bf16[4,512,8,64]{1,3,2,0:T(8,128)(2,1)} %bitcast.184, bf16[4,8,512,512]{2,3,1,0:T(8,128)(2,1)} %multiply_convert_fusion), kind=kOutput, calls=%fused_computation.43 | convolution fusion | flops 1075838976 | bytes 20971520 | tf_op jit(solution)/shard_map/shqk,sqhd->skhd/dot_general | solution.py:233
  466.5 10.6 %multiply_convert_fusion.4 = bf16[4,8,64,512]{3,2,1,0:T(8,128)(2,1)} fusion(bf16[4,512,8,64]{1,3,2,0:T(8,128)(2,1)} %bitcast.182, bf16[4,8,512,512]{2,3,1,0:T(8,128)(2,1)} %multiply_convert_fusion), kind=kOutput, calls=%fused_computation.44 | convolution fusion | flops 1075838976 | bytes 20971520 | tf_op jit(solution)/shard_map/shqk,skhd->sqhd/dot_general | solution.py:229
  507.2 6.3 fusion.26
  514.6 27.3 %scatter_custom_fusion.1 = f32[8320,256]{1,0:T(8,128)} fusion(s32[4160]{0:T(1024)} %copy-done.28, f32[64,256]{1,0:T(8,128)S(1)} %convert_reduce_fusion, f32[]{:T(128)} %constant.48.clone.1, f32[2048,256]{1,0:T(8,128)} %convert_multiply_fusion.4, f32[2048,256]{1,0:T(8,128)} %bitcast.174, f32[]{:T(128)} %constant.43.clone.1), kind=kCustom, calls=%fused_computation.35 | custom fusion | flops 2129920 | bytes 12780544 | tf_op jit(solution)/shard_map/scatter | solution.py:271
  547.2 6.1 all-to-all-start.3
  559.8 7.6 fusion.41
  575.2 63.3 %all-to-all-done.3 = bf16[16,520,256]{2,1,0:T(8,128)(2,1)} async-done(((bf16[16,520,256]{2,1,0:T(8,128)(2,1)}), bf16[16,520,256]{2,1,0:T(8,128)(2,1)}, u32[]{:S(2)}, u32[]{:S(2)}) %all-to-all-start.3) | async-done | bytes 4259872 | tf_op jit(solution)/shard_map/all_to_all | solution.py:273
  638.5 7.1 convert_select_fusion
  645.6 52.6 %scatter_custom_fusion.2 = f32[3125,256]{1,0:T(8,128)S(1)} fusion(s32[8320]{0:T(1024)S(1)} %reshape.563, f32[8320,256]{1,0:T(8,128)} %bitcast.180, f32[]{:T(128)} %constant.43.clone.1), kind=kCustom, calls=%fused_computation.82 | custom fusion | flops 2129920 | bytes 3200512 | tf_op jit(solution)/shard_map/scatter-add | solution.py:283
  701.4 76.3 %all-reduce.5.cloned.1.call-done = bf16[3125,256]{1,0:T(8,128)(2,1)} async-done(((bf16[3125,256]{1,0:T(8,128)(2,1)}), bf16[3125,256]{1,0:T(8,128)(2,1)}) %all-reduce.5.cloned.1.call-update) | async-done | bytes 1600016 | tf_op jit(solution)/shard_map/psum | solution.py:284
  782.0 39.6 %all-reduce.2 = (f32[]{:T(128)}, f32[]{:T(128)}, f32[3,256]{1,0:T(4,128)S(1)}) all-reduce(f32[]{:T(128)} %get-tuple-element.72, f32[]{:T(128)S(6)} %add.230, f32[3,256]{1,0:T(4,128)S(1)} %pad_maximum_fusion.3), channel_id=1, replica_groups=mesh['grp'=2,'row'=16] {'grp','row'}, use_global_device_ids=true, to_apply=%region_13.14 | all-reduce | flops 770 | bytes 6160 | tf_op jit(solution)/shard_map/psum | solution.py:170
  (212 shorter events, 159.3 us)
Async XLA Ops:
  7.2 9.3 %copy-start.44 = (s32[64]{0:T(128)S(1)}, s32[64]{0:T(128)}, u32[]{:S(2)}) copy-start(s32[64]{0:T(128)} %param.18) | copy-start | bytes 772
  16.7 173.2 %copy-start.28 = (s32[4160]{0:T(1024)}, s32[4160]{0:T(1024)S(1)}, u32[]{:S(2)}) copy-start(s32[4160]{0:T(1024)S(1)} %fusion.57) | copy-start | bytes 49924
  38.0 14.1 %all-to-all-start = ((s32[16,1,520]{2,1,0:T(1,128)}), s32[16,1,520]{2,1,0:T(1,128)S(1)}, u32[]{:S(2)}, u32[]{:S(2)}) async-start(s32[16,1,520]{2,1,0:T(1,128)} %all_to_all.15), calls=%async_computation | async-start | bytes 81920 | tf_op jit(solution)/shard_map/all_to_all | solution.py:106
  83.0 106.9 %copy-start.34 = (bf16[4,512]{1,0:T(4,128)(2,1)S(1)}, bf16[4,512]{1,0:T(4,128)(2,1)}, u32[]{:S(2)}) copy-start(bf16[4,512]{1,0:T(4,128)(2,1)} %param.17) | copy-start | bytes 12292
  83.0 107.0 %copy-start.35 = (f32[3,256]{1,0:T(4,128)S(1)}, f32[3,256]{1,0:T(4,128)}, u32[]{:S(2)}) copy-start(f32[3,256]{1,0:T(4,128)} %param.25) | copy-start | bytes 9220
  83.0 108.0 %all-to-all-start.1 = ((bf16[16,520,256]{2,1,0:T(8,128)(2,1)}), bf16[16,520,256]{2,1,0:T(8,128)(2,1)}, u32[]{:S(2)}, u32[]{:S(2)}) async-start(bf16[16,520,256]{2,1,0:T(8,128)(2,1)} %broadcast_select_fusion), calls=%async_computation.1 | async-start | bytes 8519680 | tf_op jit(solution)/shard_map/all_to_all | solution.py:110
  87.7 102.3 %all-gather.2.cloned.1.call-start = ((), (), s32[]{:S(2)}) async-start(), calls=%async_computation.5 | async-start | bytes 2433024 | tf_op jit(solution)/shard_map/all_gather | solution.py:88
  190.0 56.1 %copy-start.37 = (f32[1,256]{1,0:T(1,128)}, f32[1,256]{1,0:T(1,128)S(1)}, u32[]{:S(2)}) copy-start(f32[1,256]{1,0:T(1,128)S(1)} %get-tuple-element.100) | copy-start | bytes 3076
  191.0 106.2 %copy-start.9 = (f32[512,256]{1,0:T(8,128)}, f32[512,256]{1,0:T(8,128)S(1)}, u32[]{:S(2)}) copy-start(f32[512,256]{1,0:T(8,128)S(1)} %convert_bitcast_fusion) | copy-start | bytes 1572868
  203.6 42.5 %copy-start.2 = (bf16[4160,256]{1,0:T(8,128)(2,1)}, bf16[4160,256]{1,0:T(8,128)(2,1)S(1)}, u32[]{:S(2)}) copy-start(bf16[4160,256]{1,0:T(8,128)(2,1)S(1)} %gather_fusion.1) | copy-start | bytes 6389764
  205.6 43.7 %copy-start.29 = (f32[4,512]{1,0:T(4,128)}, f32[4,512]{1,0:T(4,128)S(1)}, u32[]{:S(2)}) copy-start(f32[4,512]{1,0:T(4,128)S(1)} %add.216) | copy-start | bytes 24580
  205.6 43.7 %copy-start.31 = (f32[4,512]{1,0:T(4,128)}, f32[4,512]{1,0:T(4,128)S(1)}, u32[]{:S(2)}) copy-start(f32[4,512]{1,0:T(4,128)S(1)} %rsqrt.30) | copy-start | bytes 24580
  255.0 8.7 %copy-start.15 = (bf16[4,512,512]{1,2,0:T(8,128)(2,1)}, bf16[4,512,512]{1,2,0:T(8,128)(2,1)S(1)}, u32[]{:S(2)}) copy-start(bf16[4,512,512]{1,2,0:T(8,128)(2,1)S(1)} %copy.151) | copy-start | bytes 6291460
  365.4 8.0 slice-start
  369.0 13.8 %copy-start.7 = (f32[2048,256]{1,0:T(8,128)}, f32[2048,256]{1,0:T(8,128)S(1)}, u32[]{:S(2)}) copy-start(f32[2048,256]{1,0:T(8,128)S(1)} %convolution_add_fusion) | copy-start | bytes 6291460
  477.1 36.4 %all-to-all-start.2 = ((bf16[16,64,256]{2,1,0:T(8,128)(2,1)}), bf16[16,64,256]{2,1,0:T(8,128)(2,1)}, u32[]{:S(2)}, u32[]{:S(2)}) async-start(bf16[16,64,256]{2,1,0:T(8,128)(2,1)} %bitcast.39), calls=%async_computation.2 | async-start | bytes 1048576 | tf_op jit(solution)/shard_map/all_to_all | solution.py:28
  547.2 91.3 %all-to-all-start.3 = ((bf16[16,520,256]{2,1,0:T(8,128)(2,1)}), bf16[16,520,256]{2,1,0:T(8,128)(2,1)}, u32[]{:S(2)}, u32[]{:S(2)}) async-start(bf16[16,520,256]{2,1,0:T(8,128)(2,1)} %bitcast.179), calls=%async_computation.3 | async-start | bytes 8519680 | tf_op jit(solution)/shard_map/all_to_all | solution.py:273
  553.3 146.3 %reduce-scatter.4.cloned.1.call-start = ((), (), s32[]{:S(2)}) async-start(), calls=%async_computation.7 | async-start | bytes 4866048
  574.3 64.2 %copy-start.27 = (pred[16,520]{1,0:T(8,128)(4,1)S(1)}, pred[16,520]{1,0:T(8,128)(4,1)}, u32[]{:S(2)}) copy-start(pred[16,520]{1,0:T(8,128)(4,1)} %copy-done.26) | copy-start | bytes 24964
  574.3 203.4 %all-reduce.5.cloned.1.call-start = ((), (), s32[]{:S(2)}) async-start(), calls=%async_computation.6 | async-start | bytes 3203072 | tf_op jit(solution)/shard_map/psum | solution.py:284
  699.6 125.3 %copy-start.36 = (f32[3,256]{1,0:T(4,128)S(1)}, f32[3,256]{1,0:T(4,128)}, u32[]{:S(2)}) copy-start(f32[3,256]{1,0:T(4,128)} %param.25) | copy-start | bytes 9220
  699.6 125.3 %copy-start.40 = (f32[3,256]{1,0:T(4,128)S(1)}, f32[3,256]{1,0:T(4,128)}, u32[]{:S(2)}) copy-start(f32[3,256]{1,0:T(4,128)} %param.26) | copy-start | bytes 9220
  699.6 125.3 %copy-start.41 = (f32[3,256]{1,0:T(4,128)S(1)}, f32[3,256]{1,0:T(4,128)}, u32[]{:S(2)}) copy-start(f32[3,256]{1,0:T(4,128)} %param.27) | copy-start | bytes 9220
  777.7 47.8 %copy-start.17 = (bf16[3125,256]{1,0:T(8,128)(2,1)S(1)}, bf16[3125,256]{1,0:T(8,128)(2,1)}, u32[]{:S(2)}) copy-start(bf16[3125,256]{1,0:T(8,128)(2,1)} %all-reduce.5.cloned.1.call-done) | copy-start | bytes 4800004
  (32 other events, 103.3 us)
Sparse Core Ops, SparseCore 0:
  92.0 97.0 all-gather.1
  574.4 113.9 reduce-scatter.3
  699.7 77.9 all-reduce.4
where the time goes:
time: 849 us; the launch traced here: 841 us
  blocking collectives  219 us (26%)
  other arithmetic  171 us (20%)
  matrix products  154 us (18%)
  waiting for transfers between devices  144 us (17%)
  local copies, waits for them, and re-layouts  107 us (13%)
  starting transfers between devices  23.7 us (3%)
  between operations  22.5 us (3%)
    unnamed x1, blocking collectives  99.9 us
    psum x2, blocking collectives, shards(): lax.psum((loss_local, event_local), ('grp', 'row'))  78.5 us
    psum x1, waiting for transfers between devices, shards(): lax.psum(owner_grad.astype(jnp.bfloat16), 'grp').astype(jnp.float32)  76.3 us
    all_to_all x1, waiting for transfers between devices, shards(): lax.all_to_all(sent_grads.reshape(peer_count, capacity, model_width).asty...  63.3 us
    scatter-add x1, other arithmetic, shards(): owner_grad = jax.ops.segment_sum(arrived, local_rows, num_segments=rows_dev)  52.6 us
    all_gather x1, blocking collectives, shards(): lax.all_gather(own_negatives, 'row', axis=0, tiled=True)  40.4 us
    convert_element_type x1, other arithmetic, shards(): (attn_probs * (d_probs - jnp.sum(attn_probs * d_probs, -1, keepdims=True)...  27.6 us
    scatter x1, other arithmetic, shards(): jnp.zeros((peer_count * capacity, model_width), single_float).at[slot_at]  27.3 us
  transfers between devices with their start and end apart: 7, of which 3 were waited for; matrix products, arithmetic and copies ran while one was open for 14% of the time, Pallas kernels for 0%

commit v1 on v0

--- a/solution.py
+++ b/solution.py
@@ -15,6 +15,29 @@
 beta_two = 0.999
 adam_eps = 1e-08
 decay_rate = 0.01
+
+
+def cut_along(x, dim, devices):
+    shape = x.shape
+    parts = x.reshape(*shape[:dim], devices, shape[dim] // devices, *shape[dim + 1 :])
+    return jnp.moveaxis(parts, dim, 0)
+
+
+def laid_out(pieces, dim):
+    pieces = jnp.moveaxis(pieces, 0, dim)
+    shape = pieces.shape
+    return pieces.reshape(*shape[:dim], shape[dim] * shape[dim + 1], *shape[dim + 2 :])
+
+
+def sent_to_each(array, axis, split_dim, concat_dim):
+    size, mine = (lax.axis_size(axis), lax.axis_index(axis))
+    parts = cut_along(array, split_dim, size)
+    done = [parts[mine]]
+    for step in range(1, size):
+        sent = parts[(mine + step) % size]
+        done.append(lax.ppermute(sent, axis, [(i, (i + step) % size) for i in range(size)]))
+    parts = jnp.stack(done)[(mine - jnp.arange(size)) % size]
+    return laid_out(parts, concat_dim)
 
 
 def in_blocks(array, dim, devices):
@@ -270,12 +293,8 @@
     sent_grads = (
         jnp.zeros((peer_count * capacity, model_width), single_float).at[slot_at].set(row_grads)
     )
-    arrived = lax.all_to_all(
-        sent_grads.reshape(peer_count, capacity, model_width).astype(jnp.bfloat16),
-        "row",
-        split_axis=0,
-        concat_axis=0,
-        tiled=True,
+    arrived = sent_to_each(
+        sent_grads.reshape(peer_count, capacity, model_width).astype(jnp.bfloat16), "row", 0, 0
     ).astype(jnp.float32)
     present = asked_ids >= 0
     local_rows = jnp.where(present, asked_ids - row_base, 0).reshape(-1)

time: 849 us -> 970 us (1.14)
  waiting for transfers between devices: 144 us -> 237 us
  local copies, waits for them, and re-layouts: 107 us -> 125 us
    unnamed x4, waiting for transfers between devices: 0.08 us -> 109 us
    ppermute x0 -> x15, waiting for transfers between devices: none -> 88.7 us  [sent_to_each(): lax.ppermute(sent, axis, [(i, (i + step) % size) for i in range(size)])]
    all_to_all x1 -> x0, waiting for transfers between devices: 63.3 us -> none  [shards(): lax.all_to_all(sent_grads.reshape(peer_count, capacity, model_width).asty...]
    psum x1, waiting for transfers between devices: 76.3 us -> 34.8 us  [shards(): lax.psum(owner_grad.astype(jnp.bfloat16), 'grp').astype(jnp.float32)]
    scatter-add x1, other arithmetic: 52.6 us -> 68.8 us  [shards(): owner_grad = jax.ops.segment_sum(arrived, local_rows, num_segments=rows_dev)]
    ppermute x0 -> x15, starting transfers between devices: none -> 11.4 us  [sent_to_each(): lax.ppermute(sent, axis, [(i, (i + step) % size) for i in range(size)])]
    unnamed x112 -> x129, local copies, waits for them, and re-layouts: 18.7 us -> 29.9 us
  transfers between devices with their start and end apart: 7 -> 21, of which waited for: 3 -> 11; matrix products, arithmetic and copies ran while one was open for 14% -> 7% of each run, Pallas kernels for 0% -> 0%
where the time goes in v1:
time: 970 us; the launch traced here: 963 us
  waiting for transfers between devices  237 us (24%)
  blocking collectives  219 us (23%)
  other arithmetic  178 us (18%)
  matrix products  151 us (16%)
  local copies, waits for them, and re-layouts  125 us (13%)
  starting transfers between devices  28.7 us (3%)
  between operations  22.9 us (2%)
    unnamed x4, waiting for transfers between devices  109 us
    unnamed x1, blocking collectives  99.7 us
    ppermute x15, waiting for transfers between devices, sent_to_each(): lax.ppermute(sent, axis, [(i, (i + step) % size) for i in range(size)])  88.7 us
    psum x2, blocking collectives, shards(): lax.psum((loss_local, event_local), ('grp', 'row'))  78.9 us
    scatter-add x1, other arithmetic, shards(): owner_grad = jax.ops.segment_sum(arrived, local_rows, num_segments=rows_dev)  68.8 us
    all_gather x1, blocking collectives, shards(): lax.all_gather(own_negatives, 'row', axis=0, tiled=True)  40.6 us
    psum x1, waiting for transfers between devices, shards(): lax.psum(owner_grad.astype(jnp.bfloat16), 'grp').astype(jnp.float32)  34.8 us
    unnamed x129, local copies, waits for them, and re-layouts  29.9 us
  transfers between devices with their start and end apart: 21, of which 11 were waited for; matrix products, arithmetic and copies ran while one was open for 7% of the time, Pallas kernels for 0%

profile of v1, /device:TPU:0, one launch (start us, length us, event | category | flops | bytes accessed | tf_op | source)
XLA Modules:
  0.0 963.0 jit_solution(7782218380410821610)
XLA Ops:
  16.7 20.6 %scatter_custom_fusion = s32[8320]{0:T(1024)S(1)} fusion(s32[4160]{0:T(1024)S(1)} %fusion.58, s32[4160]{0:T(1024)S(1)} %constant_dynamic-update-slice_fusion.1, s32[]{:T(128)} %constant.171.clone.1), kind=kCustom, calls=%fused_computation.152 | custom fusion | bytes 33284 | tf_op jit(solution)/shard_map/scatter | solution.py:125
  52.2 24.2 %gather_fusion = bf16[8320,256]{1,0:T(8,128)(2,1)} fusion(bf16[3125,256]{1,0:T(8,128)(2,1)S(1)} %convert_element_type.136, s32[9216]{0:T(1024)S(1)} %pad_clamp_fusion), kind=kCustom, calls=%fused_computation | custom fusion | bytes 8552960 | tf_op jit(solution)/shard_map/gather | solution.py:131
  88.9 99.7 %all-reduce.1 = bf16[1024]{0:T(1024)(128)(2,1)S(1)} all-reduce(bf16[1024]{0:T(1024)(128)(2,1)S(1)} %dynamic-update-slice), channel_id=1, replica_groups=mesh['grp'=2,'row'=16] {'row'}, use_global_device_ids=true, to_apply=%add.1 | all-reduce | flops 1024 | bytes 4096
  191.9 12.5 %gather_fusion.1 = bf16[4160,256]{1,0:T(8,128)(2,1)S(1)} fusion(bf16[8320,256]{1,0:T(8,128)(2,1)} %bitcast.5, s32[5120]{0:T(1024)S(1)} %pad_clamp_fusion.1), kind=kCustom, calls=%fused_computation.1 | custom fusion | bytes 4276480 | tf_op jit(solution)/shard_map/gather | solution.py:135
  206.5 40.6 %all_gather.10 = bf16[1024,256]{1,0:T(8,128)(2,1)} all-gather(bf16[64,256]{1,0:T(8,128)(2,1)S(1)} %slice.86), channel_id=1, replica_groups=mesh['grp'=2,'row'=16] {'row'}, dimensions={0}, use_global_device_ids=true | all-gather | bytes 557056 | tf_op jit(solution)/shard_map/all_gather | solution.py:140
  264.7 19.1 %fusion.75 = (f32[4,8,512]{2,1,0:T(8,128)S(1)}, f32[4,8,512,512]{2,3,1,0:T(8,128)}) fusion(pred[512,512]{0,1:T(8,128)(4,1)S(1)} %iota_compare_fusion, bf16[4,512,8,64]{1,3,2,0:T(8,128)(2,1)} %bitcast.221, bf16[4,512,8,64]{1,3,2,0:T(8,128)(2,1)S(1)} %bitcast.219), kind=kOutput, calls=%fused_computation.213 | convolution fusion | flops 1107296768 | bytes 38076416 | tf_op jit(solution)/shard_map/sub | solution.py:83
  283.8 14.7 %fusion.36 = bf16[4,8,64,512]{3,2,1,0:T(8,128)(2,1)} fusion(bf16[4,512,8,64]{1,3,2,0:T(8,128)(2,1)} %bitcast.231, f32[4,8,512,512]{2,3,1,0:T(8,128)} %get-tuple-element.118, f32[4,8,512]{2,1,0:T(8,128)S(1)} %get-tuple-element.117), kind=kOutput, calls=%fused_computation.82 | convolution fusion | flops 1091567616 | bytes 37814272 | tf_op jit(solution)/shard_map/shqk,skhd->sqhd/dot_general | solution.py:157
  322.5 38.8 %psum.43 = f32[]{:T(128)} all-reduce(f32[]{:T(128)} %get-tuple-element.71), channel_id=1, replica_groups=mesh['grp'=2,'row'=16] {'grp','row'}, use_global_device_ids=true, to_apply=%region_15.16 | all-reduce | flops 1 | bytes 8 | tf_op jit(solution)/shard_map/psum | solution.py:193
  388.6 15.3 %fusion.39 = bf16[4,8,64,512]{3,2,1,0:T(8,128)(2,1)} fusion(bf16[4,512,8,64]{1,3,2,0:T(8,128)(2,1)} %bitcast.234, f32[4,8,512,512]{2,3,1,0:T(8,128)} %get-tuple-element.118, f32[4,8,512]{2,1,0:T(8,128)S(1)} %get-tuple-element.117), kind=kOutput, calls=%fused_computation.83 | convolution fusion | flops 1091567616 | bytes 37814272 | tf_op jit(solution)/shard_map/shqk,sqhd->skhd/dot_general | solution.py:242
  403.9 22.7 %multiply_reduce_fusion = (f32[4,8,512]{2,1,0:T(8,128)S(1)}, f32[4,8,512,512]{2,3,1,0:T(8,128)}) fusion(f32[4,8,512,512]{2,3,1,0:T(8,128)} %get-tuple-element.118, f32[4,8,512]{2,1,0:T(8,128)S(1)} %get-tuple-element.117, bf16[4,512,8,64]{1,3,2,0:T(8,128)(2,1)} %bitcast.235, bf16[4,512,8,64]{1,3,2,0:T(8,128)(2,1)} %bitcast.232), kind=kOutput, calls=%fused_computation.8 | convolution fusion | flops 1098891264 | bytes 71434240 | tf_op jit(solution)/shard_map/sqhd,skhd->shqk/dot_general | solution.py:245
  426.5 27.6 %multiply_convert_fusion = bf16[4,8,512,512]{2,3,1,0:T(8,128)(2,1)} fusion(f32[4,8,512,512]{2,3,1,0:T(8,128)} %get-tuple-element.127, f32[4,8,512]{2,1,0:T(8,128)S(1)} %get-tuple-element.126, f32[4,8,512,512]{2,3,1,0:T(8,128)} %get-tuple-element.118, f32[4,8,512]{2,1,0:T(8,128)S(1)} %get-tuple-element.117), kind=kLoop, calls=%fused_computation.7 | loop fusion | flops 33554432 | bytes 84017152 | tf_op jit(solution)/shard_map/convert_element_type | solution.py:248
  454.2 12.9 %multiply_convert_fusion.3 = bf16[4,8,64,512]{3,2,1,0:T(8,128)(2,1)} fusion(bf16[4,512,8,64]{1,3,2,0:T(8,128)(2,1)} %bitcast.222, bf16[4,8,512,512]{2,3,1,0:T(8,128)(2,1)} %multiply_convert_fusion), kind=kOutput, calls=%fused_computation.47 | convolution fusion | flops 1075838976 | bytes 20971520 | tf_op jit(solution)/shard_map/shqk,sqhd->skhd/dot_general | solution.py:256
  467.1 10.6 %multiply_convert_fusion.4 = bf16[4,8,64,512]{3,2,1,0:T(8,128)(2,1)} fusion(bf16[4,512,8,64]{1,3,2,0:T(8,128)(2,1)} %bitcast.220, bf16[4,8,512,512]{2,3,1,0:T(8,128)(2,1)} %multiply_convert_fusion), kind=kOutput, calls=%fused_computation.48 | convolution fusion | flops 1075838976 | bytes 20971520 | tf_op jit(solution)/shard_map/shqk,skhd->sqhd/dot_general | solution.py:252
  508.1 27.3 %scatter_custom_fusion.1 = f32[8320,256]{1,0:T(8,128)} fusion(s32[4160]{0:T(1024)} %copy-done.28, f32[64,256]{1,0:T(8,128)S(1)} %convert_reduce_fusion, f32[]{:T(128)} %constant.185.clone.1, f32[2048,256]{1,0:T(8,128)} %convert_multiply_fusion.4, f32[2048,256]{1,0:T(8,128)} %bitcast.211, f32[]{:T(128)} %constant.180.clone.1), kind=kCustom, calls=%fused_computation.37 | custom fusion | flops 2129920 | bytes 12780544 | tf_op jit(solution)/shard_map/scatter | solution.py:294
  552.2 10.0 %collective-permute-done.1 = bf16[1,520,256]{2,1,0:T(8,128)(2,1)S(1)} collective-permute-done((bf16[1,520,256]{2,1,0:T(8,128)(2,1)S(1)}, bf16[1,520,256]{2,1,0:T(8,128)(2,1)S(1)}, u32[]{:S(2)}, u32[]{:S(2)}) %collective-permute-start.1) | collective-permute-done | bytes 266272 | tf_op jit(solution)/shard_map/ppermute | solution.py:38
  574.8 18.6 %collective-permute-done.4 = bf16[1,520,256]{2,1,0:T(8,128)(2,1)S(1)} collective-permute-done((bf16[1,520,256]{2,1,0:T(8,128)(2,1)S(1)}, bf16[1,520,256]{2,1,0:T(8,128)(2,1)S(1)}, u32[]{:S(2)}, u32[]{:S(2)}) %collective-permute-start.4) | collective-permute-done | bytes 266272 | tf_op jit(solution)/shard_map/ppermute | solution.py:38
  594.8 22.3 %collective-permute-done.6 = bf16[1,520,256]{2,1,0:T(8,128)(2,1)S(1)} collective-permute-done((bf16[1,520,256]{2,1,0:T(8,128)(2,1)S(1)}, bf16[1,520,256]{2,1,0:T(8,128)(2,1)S(1)}, u32[]{:S(2)}, u32[]{:S(2)}) %collective-permute-start.6) | collective-permute-done | bytes 266272 | tf_op jit(solution)/shard_map/ppermute | solution.py:38
  618.6 8.8 collective-permute-done.8
  630.5 15.3 %collective-permute-done.10 = bf16[1,520,256]{2,1,0:T(8,128)(2,1)S(1)} collective-permute-done((bf16[1,520,256]{2,1,0:T(8,128)(2,1)S(1)}, bf16[1,520,256]{2,1,0:T(8,128)(2,1)S(1)}, u32[]{:S(2)}, u32[]{:S(2)}) %collective-permute-start.10) | collective-permute-done | bytes 266272 | tf_op jit(solution)/shard_map/ppermute | solution.py:38
  659.4 68.8 %scatter_custom_fusion.2 = f32[3125,256]{1,0:T(8,128)} fusion(s32[8320]{0:T(1024)} %reshape.661, bf16[8320,256]{1,0:T(8,128)(2,1)} %bitcast.216, f32[]{:T(128)} %constant.180.clone.1, pred[8320]{0:T(1024)(128)(4,1)S(1)} %copy-done.33), kind=kCustom, calls=%fused_computation.19 | custom fusion | flops 6389760 | bytes 7469184 | tf_op jit(solution)/shard_map/scatter-add | solution.py:302
  738.3 7.5 fusion.43
  753.4 34.8 %all-reduce.5.cloned.1.call-done = bf16[3125,256]{1,0:T(8,128)(2,1)} async-done(((bf16[3125,256]{1,0:T(8,128)(2,1)}), bf16[3125,256]{1,0:T(8,128)(2,1)}) %all-reduce.5.cloned.1.call-update) | async-done | bytes 1600016 | tf_op jit(solution)/shard_map/psum | solution.py:303
  791.9 109.2 %reduce-scatter.4.cloned.1.call-done = f32[144,256]{1,0:T(8,128)} async-done(((f32[4608,256]{1,0:T(8,128)}), f32[144,256]{1,0:T(8,128)}) %reduce-scatter.4.cloned.1.call-update) | async-done | bytes 147472
  903.5 40.1 %all-reduce.2 = (f32[]{:T(128)}, f32[]{:T(128)}, f32[3,256]{1,0:T(4,128)S(1)}) all-reduce(f32[]{:T(128)} %get-tuple-element.72, f32[]{:T(128)S(6)} %add.440, f32[3,256]{1,0:T(4,128)S(1)} %pad_maximum_fusion.3), channel_id=1, replica_groups=mesh['grp'=2,'row'=16] {'grp','row'}, use_global_device_ids=true, to_apply=%region_13.14 | all-reduce | flops 770 | bytes 6160 | tf_op jit(solution)/shard_map/psum | solution.py:193
  (261 shorter events, 218.2 us)
Async XLA Ops:
  38.0 14.1 %all-to-all-start = ((s32[16,1,520]{2,1,0:T(1,128)}), s32[16,1,520]{2,1,0:T(1,128)S(1)}, u32[]{:S(2)}, u32[]{:S(2)}) async-start(s32[16,1,520]{2,1,0:T(1,128)} %all_to_all.12), calls=%async_computation | async-start | bytes 81920 | tf_op jit(solution)/shard_map/all_to_all | solution.py:129
  81.8 110.1 %all-to-all-start.1 = ((bf16[16,520,256]{2,1,0:T(8,128)(2,1)}), bf16[16,520,256]{2,1,0:T(8,128)(2,1)}, u32[]{:S(2)}, u32[]{:S(2)}) async-start(bf16[16,520,256]{2,1,0:T(8,128)(2,1)} %broadcast_select_fusion), calls=%async_computation.1 | async-start | bytes 8519680 | tf_op jit(solution)/shard_map/all_to_all | solution.py:133
  86.5 104.4 %all-gather.2.cloned.1.call-start = ((), (), s32[]{:S(2)}) async-start(), calls=%async_computation.4 | async-start | bytes 2433024 | tf_op jit(solution)/shard_map/all_gather | solution.py:111
  477.6 30.4 %all-to-all-start.2 = ((bf16[16,64,256]{2,1,0:T(8,128)(2,1)}), bf16[16,64,256]{2,1,0:T(8,128)(2,1)S(1)}, u32[]{:S(2)}, u32[]{:S(2)}) async-start(bf16[16,64,256]{2,1,0:T(8,128)(2,1)} %bitcast.39), calls=%async_computation.2 | async-start | bytes 1048576 | tf_op jit(solution)/shard_map/all_to_all | solution.py:51
  482.8 305.5 %all-reduce.5.cloned.1.call-start = ((), (), s32[]{:S(2)}) async-start(), calls=%async_computation.5 | async-start | bytes 3203072 | tf_op jit(solution)/shard_map/psum | solution.py:303
  539.5 10.7 %collective-permute-start = (bf16[1,520,256]{2,1,0:T(8,128)(2,1)S(1)}, bf16[1,520,256]{2,1,0:T(8,128)(2,1)S(1)}, u32[]{:S(2)}, u32[]{:S(2)}) collective-permute-start(bf16[1,520,256]{2,1,0:T(8,128)(2,1)S(1)} %get-tuple-element.113), channel_id=1, source_target_pairs={{0,1},{1,2},{2,3},{3,4},{4,5},{5,6},{6,7},{7,8},{8,9},{9,10},{10,1... | collective-permute-start | bytes 798728 | tf_op jit(solution)/shard_map/ppermute | solution.py:38
  543.0 19.3 %collective-permute-start.1 = (bf16[1,520,256]{2,1,0:T(8,128)(2,1)S(1)}, bf16[1,520,256]{2,1,0:T(8,128)(2,1)S(1)}, u32[]{:S(2)}, u32[]{:S(2)}) collective-permute-start(bf16[1,520,256]{2,1,0:T(8,128)(2,1)S(1)} %get-tuple-element.112), channel_id=1, source_target_pairs={{0,2},{1,3},{2,4},{3,5},{4,6},{5,7},{6,8},{7,9},{8,10},{9,11},{10,... | collective-permute-start | bytes 798728 | tf_op jit(solution)/shard_map/ppermute | solution.py:38
  545.6 107.9 %collective-permute-start.14 = (bf16[1,520,256]{2,1,0:T(8,128)(2,1)S(1)}, bf16[1,520,256]{2,1,0:T(8,128)(2,1)S(1)}, u32[]{:S(2)}, u32[]{:S(2)}) collective-permute-start(bf16[1,520,256]{2,1,0:T(8,128)(2,1)S(1)} %get-tuple-element.99), channel_id=1, source_target_pairs={{0,15},{1,0},{2,1},{3,2},{4,3},{5,4},{6,5},{7,6},{8,7},{9,8},{10,9... | collective-permute-start | bytes 798728 | tf_op jit(solution)/shard_map/ppermute | solution.py:38
  548.1 104.7 %collective-permute-start.13 = (bf16[1,520,256]{2,1,0:T(8,128)(2,1)S(1)}, bf16[1,520,256]{2,1,0:T(8,128)(2,1)S(1)}, u32[]{:S(2)}, u32[]{:S(2)}) collective-permute-start(bf16[1,520,256]{2,1,0:T(8,128)(2,1)S(1)} %get-tuple-element.100), channel_id=1, source_target_pairs={{0,14},{1,15},{2,0},{3,1},{4,2},{5,3},{6,4},{7,5},{8,6},{9,7},{10,... | collective-permute-start | bytes 798728 | tf_op jit(solution)/shard_map/ppermute | solution.py:38
  549.8 102.3 %collective-permute-start.12 = (bf16[1,520,256]{2,1,0:T(8,128)(2,1)S(1)}, bf16[1,520,256]{2,1,0:T(8,128)(2,1)S(1)}, u32[]{:S(2)}, u32[]{:S(2)}) collective-permute-start(bf16[1,520,256]{2,1,0:T(8,128)(2,1)S(1)} %get-tuple-element.101), channel_id=1, source_target_pairs={{0,13},{1,14},{2,15},{3,0},{4,1},{5,2},{6,3},{7,4},{8,5},{9,6},{10... | collective-permute-start | bytes 798728 | tf_op jit(solution)/shard_map/ppermute | solution.py:38
  550.2 18.4 %collective-permute-start.2 = (bf16[1,520,256]{2,1,0:T(8,128)(2,1)S(1)}, bf16[1,520,256]{2,1,0:T(8,128)(2,1)S(1)}, u32[]{:S(2)}, u32[]{:S(2)}) collective-permute-start(bf16[1,520,256]{2,1,0:T(8,128)(2,1)S(1)} %get-tuple-element.111), channel_id=1, source_target_pairs={{0,3},{1,4},{2,5},{3,6},{4,7},{5,8},{6,9},{7,10},{8,11},{9,12},{10... | collective-permute-start | bytes 798728 | tf_op jit(solution)/shard_map/ppermute | solution.py:38
  562.2 11.8 %collective-permute-start.3 = (bf16[1,520,256]{2,1,0:T(8,128)(2,1)S(1)}, bf16[1,520,256]{2,1,0:T(8,128)(2,1)S(1)}, u32[]{:S(2)}, u32[]{:S(2)}) collective-permute-start(bf16[1,520,256]{2,1,0:T(8,128)(2,1)S(1)} %get-tuple-element.110), channel_id=1, source_target_pairs={{0,4},{1,5},{2,6},{3,7},{4,8},{5,9},{6,10},{7,11},{8,12},{9,13},{1... | collective-permute-start | bytes 798728 | tf_op jit(solution)/shard_map/ppermute | solution.py:38
  568.6 24.8 %collective-permute-start.4 = (bf16[1,520,256]{2,1,0:T(8,128)(2,1)S(1)}, bf16[1,520,256]{2,1,0:T(8,128)(2,1)S(1)}, u32[]{:S(2)}, u32[]{:S(2)}) collective-permute-start(bf16[1,520,256]{2,1,0:T(8,128)(2,1)S(1)} %get-tuple-element.109), channel_id=1, source_target_pairs={{0,5},{1,6},{2,7},{3,8},{4,9},{5,10},{6,11},{7,12},{8,13},{9,14},{... | collective-permute-start | bytes 798728 | tf_op jit(solution)/shard_map/ppermute | solution.py:38
  574.1 20.1 %collective-permute-start.5 = (bf16[1,520,256]{2,1,0:T(8,128)(2,1)S(1)}, bf16[1,520,256]{2,1,0:T(8,128)(2,1)S(1)}, u32[]{:S(2)}, u32[]{:S(2)}) collective-permute-start(bf16[1,520,256]{2,1,0:T(8,128)(2,1)S(1)} %get-tuple-element.108), channel_id=1, source_target_pairs={{0,6},{1,7},{2,8},{3,9},{4,10},{5,11},{6,12},{7,13},{8,14},{9,15},... | collective-permute-start | bytes 798728 | tf_op jit(solution)/shard_map/ppermute | solution.py:38
  593.4 23.7 %collective-permute-start.6 = (bf16[1,520,256]{2,1,0:T(8,128)(2,1)S(1)}, bf16[1,520,256]{2,1,0:T(8,128)(2,1)S(1)}, u32[]{:S(2)}, u32[]{:S(2)}) collective-permute-start(bf16[1,520,256]{2,1,0:T(8,128)(2,1)S(1)} %get-tuple-element.107), channel_id=1, source_target_pairs={{0,7},{1,8},{2,9},{3,10},{4,11},{5,12},{6,13},{7,14},{8,15},{9,0},... | collective-permute-start | bytes 798728 | tf_op jit(solution)/shard_map/ppermute | solution.py:38
  594.1 23.7 %collective-permute-start.7 = (bf16[1,520,256]{2,1,0:T(8,128)(2,1)S(1)}, bf16[1,520,256]{2,1,0:T(8,128)(2,1)S(1)}, u32[]{:S(2)}, u32[]{:S(2)}) collective-permute-start(bf16[1,520,256]{2,1,0:T(8,128)(2,1)S(1)} %get-tuple-element.106), channel_id=1, source_target_pairs={{0,8},{1,9},{2,10},{3,11},{4,12},{5,13},{6,14},{7,15},{8,0},{9,1},... | collective-permute-start | bytes 798728 | tf_op jit(solution)/shard_map/ppermute | solution.py:38
  617.1 10.3 %collective-permute-start.8 = (bf16[1,520,256]{2,1,0:T(8,128)(2,1)S(1)}, bf16[1,520,256]{2,1,0:T(8,128)(2,1)S(1)}, u32[]{:S(2)}, u32[]{:S(2)}) collective-permute-start(bf16[1,520,256]{2,1,0:T(8,128)(2,1)S(1)} %get-tuple-element.105), channel_id=1, source_target_pairs={{0,9},{1,10},{2,11},{3,12},{4,13},{5,14},{6,15},{7,0},{8,1},{9,2},... | collective-permute-start | bytes 798728 | tf_op jit(solution)/shard_map/ppermute | solution.py:38
  617.8 10.3 %collective-permute-start.9 = (bf16[1,520,256]{2,1,0:T(8,128)(2,1)S(1)}, bf16[1,520,256]{2,1,0:T(8,128)(2,1)S(1)}, u32[]{:S(2)}, u32[]{:S(2)}) collective-permute-start(bf16[1,520,256]{2,1,0:T(8,128)(2,1)S(1)} %get-tuple-element.104), channel_id=1, source_target_pairs={{0,10},{1,11},{2,12},{3,13},{4,14},{5,15},{6,0},{7,1},{8,2},{9,3},... | collective-permute-start | bytes 798728 | tf_op jit(solution)/shard_map/ppermute | solution.py:38
  627.4 18.4 %collective-permute-start.10 = (bf16[1,520,256]{2,1,0:T(8,128)(2,1)S(1)}, bf16[1,520,256]{2,1,0:T(8,128)(2,1)S(1)}, u32[]{:S(2)}, u32[]{:S(2)}) collective-permute-start(bf16[1,520,256]{2,1,0:T(8,128)(2,1)S(1)} %get-tuple-element.103), channel_id=1, source_target_pairs={{0,11},{1,12},{2,13},{3,14},{4,15},{5,0},{6,1},{7,2},{8,3},{9,4},{... | collective-permute-start | bytes 798728 | tf_op jit(solution)/shard_map/ppermute | solution.py:38
  628.1 23.2 %collective-permute-start.11 = (bf16[1,520,256]{2,1,0:T(8,128)(2,1)S(1)}, bf16[1,520,256]{2,1,0:T(8,128)(2,1)S(1)}, u32[]{:S(2)}, u32[]{:S(2)}) collective-permute-start(bf16[1,520,256]{2,1,0:T(8,128)(2,1)S(1)} %get-tuple-element.102), channel_id=1, source_target_pairs={{0,12},{1,13},{2,14},{3,15},{4,0},{5,1},{6,2},{7,3},{8,4},{9,5},{1... | collective-permute-start | bytes 798728 | tf_op jit(solution)/shard_map/ppermute | solution.py:38
  731.4 169.8 %reduce-scatter.4.cloned.1.call-start = ((), (), s32[]{:S(2)}) async-start(), calls=%async_computation.6 | async-start | bytes 4866048
  752.7 194.2 %copy-start.41 = (f32[3,256]{1,0:T(4,128)S(1)}, f32[3,256]{1,0:T(4,128)}, u32[]{:S(2)}) copy-start(f32[3,256]{1,0:T(4,128)} %param.26) | copy-start | bytes 9220
  752.7 194.2 %copy-start.42 = (f32[3,256]{1,0:T(4,128)S(1)}, f32[3,256]{1,0:T(4,128)}, u32[]{:S(2)}) copy-start(f32[3,256]{1,0:T(4,128)} %param.27) | copy-start | bytes 9220
  753.4 196.1 %copy-start.34 = (f32[3125]{0:T(1024)S(1)}, f32[3125]{0:T(1024)}, u32[]{:S(2)}) copy-start(f32[3125]{0:T(1024)} %param.21) | copy-start | bytes 37504
  (47 other events, 1202.7 us)
Sparse Core Ops, SparseCore 0:
  90.7 97.0 all-gather.1
  731.5 56.6 all-reduce.4
  793.8 107.3 reduce-scatter.3
